TPU v7x, 32 devices: a whole 2x2x4 slice. The times are simulated.
32 devices in a mesh: blk: 16 (over z, y, x), row: 2 (over core).
Axes of the slice: x: 2, y: 2, z: 4, core: 2. Of those that a mesh axis runs over, the one named last changes fastest.
Arguments:
- genotypes: bfloat16 [128, 16, 2048], P('blk', None, 'row'), may hold values from 0 to 2
- assignment: int32 [16], replicated, may hold values from 0 to 15, each once
- snp_counts: int32 [16], replicated, may hold values from 1024 to 2048, as said below
- basis: float32 [16, 64, 2048], P('blk', None, 'row'), may hold values from -6 to 6
Outputs:
- image: float32 [16, 64, 2048], P('blk', None, 'row')
- new_basis: float32 [16, 64, 2048], P('blk', None, 'row')
- factor: float32 [16, 64, 64], P('blk')
Inputs may be any that keep to these rules, and one draw needn't show every extreme that they name: `assignment`: each block number appears exactly once. `snp_counts`: A block's SNPs fill its leading slots.
All inputs are finite; a program needn't handle non-finite values.
Results may differ from a plain program's by a relative error of at most 0.0021.
Values may be sent and summed in bfloat16 or wider, within the bound.
No kernel may reach another device: no remote copies, remote signals or barrier semaphores. Data moves between devices by JAX's collectives and lax.ppermute only.
A program may use at most 64 MiB of HBM per device.

v0:
```python
import jax
import jax.numpy as jnp
from jax import lax
from jax.sharding import PartitionSpec as P

epsilon = 1e-05
shrink_weight = 0.5


def body(genotypes, assignment, snp_counts, basis):
    ordered = jnp.take(genotypes, assignment, axis=1)
    regrouped = lax.all_to_all(ordered, "blk", split_axis=1, concat_axis=0, tiled=True)
    samples = regrouped.shape[0]
    owned = regrouped.shape[1]
    half_width = regrouped.shape[2]
    block_ids = lax.dynamic_slice_in_dim(assignment, lax.axis_index("blk") * owned, owned)
    catalog = jnp.arange(snp_counts.shape[0], dtype=jnp.int32)
    live_count = jnp.sum(
        jnp.where(block_ids[:, None] == catalog[None, :], snp_counts[None, :], 0), axis=1
    )
    columns = lax.axis_index("row") * half_width + jnp.arange(half_width, dtype=jnp.int32)
    live_mask = columns[None, :] < live_count[:, None]
    values = regrouped.astype(jnp.float32)
    col_mean = jnp.mean(values, axis=0)
    centered = values - col_mean[None]
    col_var = jnp.mean(centered * centered, axis=0)
    standard = jnp.where(
        live_mask[None], centered * lax.rsqrt(col_var + epsilon)[None], 0.0
    ).astype(jnp.bfloat16)
    inverse = 1.0 / samples
    partial_proj = jnp.einsum(
        "nbi,bri->brn",
        standard,
        basis,
        precision=lax.Precision.HIGHEST,
        preferred_element_type=jnp.float32,
    )
    projected = lax.psum(partial_proj, "row")
    product = (
        jnp.einsum(
            "nbi,brn->bri",
            standard,
            projected,
            precision=lax.Precision.HIGHEST,
            preferred_element_type=jnp.float32,
        )
        * inverse
    )
    image = shrink_weight * product + (1.0 - shrink_weight) * jnp.where(
        live_mask[:, None, :], basis, 0.0
    )
    gram_part = jnp.einsum("bri,bsi->brs", image, image, precision=lax.Precision.HIGHEST)
    gram_sum = lax.psum(gram_part, "row")
    factor = jnp.linalg.cholesky(gram_sum)
    new_basis = jax.scipy.linalg.solve_triangular(factor, image, lower=True)
    return (image, new_basis, factor)


def solution(mesh):
    in_specs = (P("blk", None, "row"), P(), P(), P("blk", None, "row"))
    out_specs = (P("blk", None, "row"), P("blk", None, "row"), P("blk", None, None))
    return jax.shard_map(body, mesh=mesh, in_specs=in_specs, out_specs=out_specs, check_vma=False)
```

profile of v0, /device:TPU:0, one launch (start us, length us, event | category | flops | bytes accessed | tf_op | source)
XLA Modules:
  0.0 44.3 jit_solution(11214147400684434349)
XLA Ops:
  0.6 0.0 copy-start
  0.6 0.0 copy-start.3
  0.7 0.7 %compare_and_fusion = pred[16]{0:T(512)(128)(4,1)S(1)} fusion(s32[16]{0:T(128)} %param.5), kind=kLoop, calls=%fused_computation.36 | loop fusion | flops 96 | bytes 80 | tf_op jit(solution)/shard_map/jit(_take)/and | solution.py:11
  1.4 0.0 copy-done.3
  1.4 0.2 copy-done
  1.6 1.3 %gather_fusion = bf16[16,8,1024]{2,0,1:T(8,128)(2,1)S(1)} fusion(bf16[8,16,1024]{2,1,0:T(8,128)(2,1)S(1)} %copy-done, s32[1024]{0:T(1024)S(1)} %pad_clamp_fusion), kind=kCustom, calls=%fused_computation | custom fusion | bytes 524352 | tf_op jit(solution)/shard_map/jit(_take)/gather | solution.py:11
  2.9 0.1 select_bitcast_fusion
  3.0 0.9 %copy.13 = bf16[8,16,1024]{2,0,1:T(8,128)(2,1)} copy(bf16[8,16,1024]{2,1,0:T(8,128)(2,1)S(1)} %select_bitcast_fusion) | data formatting | bytes 524288 | tf_op jit(solution)/shard_map/jit(_take)/select_n | solution.py:11
  3.9 8.3 %all-to-all-start = ((bf16[8,16,1024]{2,0,1:T(8,128)(2,1)}), bf16[8,16,1024]{2,0,1:T(8,128)(2,1)S(1)}, u32[]{:S(2)}, u32[]{:S(2)}) async-start(bf16[8,16,1024]{2,0,1:T(8,128)(2,1)} %copy.13), calls=%async_computation | async-start | bytes 524288 | tf_op jit(solution)/shard_map/all_to_all | solution.py:12
  12.2 0.6 %dynamic_slice.3 = s32[1]{0:T(128)} dynamic-slice(s32[16]{0:T(128)S(1)} %copy-done.3, s32[]{:T(128)S(6)} %select_n.50), dynamic_slice_sizes={1} | dynamic-slice | bytes 12 | tf_op jit(solution)/shard_map/dynamic_slice | solution.py:16
  12.8 0.0 copy-start.4
  12.8 0.7 %copy-done.4 = s32[16]{0:T(128)S(1)} copy-done((s32[16]{0:T(128)S(1)}, s32[16]{0:T(128)}, u32[]{:S(2)}) %copy-start.4) | copy-done | bytes 88
  13.5 1.3 %fusion.18 = s32[]{:T(128)} fusion(s32[16]{0:T(128)S(1)} %copy-done.4, s32[]{:T(128)} %bitcast), kind=kLoop, calls=%fused_computation.38 | loop fusion | flops 47 | bytes 72 | tf_op jit(solution)/shard_map/reduce_sum | solution.py:18
  14.8 0.7 %add_compare_fusion = pred[1024]{0:T(1024)(128)(4,1)S(1)} fusion(s32[]{:T(128)} %fusion.18, s32[]{:T(128)S(6)} %mul.56), kind=kLoop, calls=%fused_computation.32 | loop fusion | flops 2048 | bytes 1032 | tf_op jit(solution)/shard_map/lt | solution.py:22
  15.4 0.0 copy-start.2
  15.4 6.7 %all-to-all-done = bf16[8,16,1024]{2,0,1:T(8,128)(2,1)S(1)} async-done(((bf16[8,16,1024]{2,0,1:T(8,128)(2,1)}), bf16[8,16,1024]{2,0,1:T(8,128)(2,1)S(1)}, u32[]{:S(2)}, u32[]{:S(2)}) %all-to-all-start) | async-done | bytes 262176 | tf_op jit(solution)/shard_map/all_to_all | solution.py:12
  22.1 0.1 convert_reduce_fusion
  22.2 0.1 fusion.4
  22.3 0.0 copy-done.2
  22.3 0.4 convolution_bitcast_fusion.2
  22.7 3.4 %psum.14 = f32[64,128]{1,0:T(8,128)S(1)} all-reduce(f32[64,128]{1,0:T(8,128)S(1)} %convolution_bitcast_fusion.2), channel_id=1, replica_groups=mesh['blk'=16,'row'=2] {'row'}, use_global_device_ids=true, to_apply=%region_3.4 | all-reduce | flops 8192 | bytes 65536 | tf_op jit(solution)/shard_map/psum | solution.py:38
  26.1 0.3 fusion.1
  26.4 0.0 copy-start.1
  26.4 0.4 convolution_bitcast_fusion.1
  26.8 3.6 %psum.15 = f32[1,64,64]{1,2,0:T(8,128)S(1)} all-reduce(f32[1,64,64]{1,2,0:T(8,128)S(1)} %convolution_bitcast_fusion.1), channel_id=1, replica_groups=mesh['blk'=16,'row'=2] {'row'}, use_global_device_ids=true, to_apply=%region_4.5 | all-reduce | flops 4096 | bytes 32768 | tf_op jit(solution)/shard_map/psum | solution.py:53
  30.3 0.1 copy.15
  30.4 5.8 %custom-call.8 = f32[1,64,64]{2,1,0:T(8,128)S(1)} custom-call(f32[1,64,64]{2,1,0:T(8,128)S(1)} %fusion.16), custom_call_target="Cholesky" | custom-call | tf_op jit(solution)/shard_map/jit(cholesky)/cholesky | solution.py:54
  36.3 0.6 %compare_reduce_fusion = pred[]{:T(512)} fusion(f32[64]{0:T(128)S(1)} %select_reduce_fusion), kind=kLoop, calls=%fused_computation.35 | loop fusion | flops 127 | bytes 257 | tf_op jit(solution)/shard_map/jit(cholesky)/cholesky | solution.py:54
  37.0 1.3 %fusion.17 = (f32[1,64,64]{2,1,0:T(8,128)S(1)}, f32[1,64,64]{2,1,0:T(8,128)}) fusion(f32[1,64,64]{2,1,0:T(8,128)S(1)} %custom-call.8, pred[]{:T(512)} %compare_reduce_fusion), kind=kLoop, calls=%fused_computation.29 | loop fusion | flops 16384 | bytes 49153 | tf_op jit(solution)/shard_map/jit(_solve_triangular)/triangular_solve | solution.py:55
  38.2 4.9 %custom-call.9 = f32[1,64,64]{1,2,0:T(8,128)S(1)} custom-call(f32[1,64,64]{2,1,0:T(8,128)S(1)} %get-tuple-element.3), custom_call_target="InvertDiagBlocksLowerTriangular" | custom-call | tf_op jit(solution)/shard_map/jit(_solve_triangular)/triangular_solve | solution.py:55
  43.1 0.0 copy-done.1
  43.1 1.1 %convolution_bitcast_fusion = f32[1,64,1024]{2,1,0:T(8,128)} fusion(f32[1,64,1024]{2,1,0:T(8,128)S(1)} %fusion.1, f32[1,64,64]{1,2,0:T(8,128)S(1)} %custom-call.9), kind=kOutput, calls=%fused_computation.3 | convolution fusion | flops 50331648 | bytes 540672 | tf_op jit(solution)/shard_map/jit(_solve_triangular)/triangular_solve | solution.py:55
  (6 shorter events, 0.1 us)
Async XLA Ops:
  0.6 1.0 %copy-start = (bf16[8,16,1024]{2,1,0:T(8,128)(2,1)S(1)}, bf16[8,16,1024]{2,1,0:T(8,128)(2,1)}, u32[]{:S(2)}) copy-start(bf16[8,16,1024]{2,1,0:T(8,128)(2,1)} %param.4) | copy-start | bytes 786436
  0.6 0.7 %copy-start.3 = (s32[16]{0:T(128)S(1)}, s32[16]{0:T(128)}, u32[]{:S(2)}) copy-start(s32[16]{0:T(128)} %param.5) | copy-start | bytes 196
  3.9 18.2 %all-to-all-start = ((bf16[8,16,1024]{2,0,1:T(8,128)(2,1)}), bf16[8,16,1024]{2,0,1:T(8,128)(2,1)S(1)}, u32[]{:S(2)}, u32[]{:S(2)}) async-start(bf16[8,16,1024]{2,0,1:T(8,128)(2,1)} %copy.13), calls=%async_computation | async-start | bytes 524288 | tf_op jit(solution)/shard_map/all_to_all | solution.py:12
  12.8 0.7 %copy-start.4 = (s32[16]{0:T(128)S(1)}, s32[16]{0:T(128)}, u32[]{:S(2)}) copy-start(s32[16]{0:T(128)} %param.6) | copy-start | bytes 196
  15.4 6.9 %copy-start.2 = (f32[1,64,1024]{2,1,0:T(8,128)S(1)}, f32[1,64,1024]{2,1,0:T(8,128)}, u32[]{:S(2)}) copy-start(f32[1,64,1024]{2,1,0:T(8,128)} %param.7) | copy-start | bytes 786436
  26.4 16.8 %copy-start.1 = (f32[1,64,1024]{2,1,0:T(8,128)}, f32[1,64,1024]{2,1,0:T(8,128)S(1)}, u32[]{:S(2)}) copy-start(f32[1,64,1024]{2,1,0:T(8,128)S(1)} %fusion.1) | copy-start | bytes 786436
where the time goes:
time: 44.6 us; the launch traced here: 44.3 us
  other arithmetic  15.6 us (35%)
  starting transfers between devices  8.34 us (19%)
  blocking collectives  6.97 us (16%)
  waiting for transfers between devices  6.68 us (15%)
  local copies, waits for them, and re-layouts  3.73 us (8%)
  matrix products  2.15 us (5%)
  between operations  0.79 us (2%)
    all_to_all x1, starting transfers between devices, body(): lax.all_to_all(ordered, 'blk', split_axis=1, concat_axis=0, tiled=True)  8.34 us
    all_to_all x1, waiting for transfers between devices, body(): lax.all_to_all(ordered, 'blk', split_axis=1, concat_axis=0, tiled=True)  6.68 us
    another operation x3, other arithmetic, body(): factor = jnp.linalg.cholesky(gram_sum)  6.52 us
    another operation x2, other arithmetic, body(): new_basis = jax.scipy.linalg.solve_triangular(factor, image, lower=True)  6.16 us
    psum x1, blocking collectives, body(): gram_sum = lax.psum(gram_part, 'row')  3.57 us
    psum x1, blocking collectives, body(): projected = lax.psum(partial_proj, 'row')  3.41 us
    gather x1, local copies, waits for them, and re-layouts, body(): ordered = jnp.take(genotypes, assignment, axis=1)  1.31 us
    reduce_sum x1, other arithmetic, body(): jnp.sum(jnp.where(block_ids[:, None] == catalog[None, :], snp_counts[None...  1.27 us
  transfers between devices with their start and end apart: 1, of which 1 were waited for; matrix products, arithmetic and copies ran while one was open for 6% of the time, Pallas kernels for 0%

commit v1 on v0

--- a/solution.py
+++ b/solution.py
@@ -9,7 +9,10 @@
 
 def body(genotypes, assignment, snp_counts, basis):
     ordered = jnp.take(genotypes, assignment, axis=1)
-    regrouped = lax.all_to_all(ordered, "blk", split_axis=1, concat_axis=0, tiled=True)
+    regrouped = jnp.concatenate(
+        lax.all_to_all(jnp.stack(jnp.split(ordered, lax.axis_size("blk"), axis=1)), "blk", 0, 0),
+        axis=0,
+    )
     samples = regrouped.shape[0]
     owned = regrouped.shape[1]
     half_width = regrouped.shape[2]

time: 44.6 us -> 54.1 us (1.21)
  local copies, waits for them, and re-layouts: 3.73 us -> 13.2 us
    unnamed x10 -> x25, local copies, waits for them, and re-layouts: 0.9 us -> 10.1 us
    select_n x1 -> x0, local copies, waits for them, and re-layouts: 0.85 us -> none  [body(): ordered = jnp.take(genotypes, assignment, axis=1)]
    select_n x2, other arithmetic: 0.1 us -> 0.82 us  [body(): ordered = jnp.take(genotypes, assignment, axis=1)]
    and x1, other arithmetic: 0.73 us -> 0.01 us  [body(): ordered = jnp.take(genotypes, assignment, axis=1)]
    another operation x0 -> x1, local copies, waits for them, and re-layouts: none -> 0.61 us  [body(): jnp.stack(jnp.split(ordered, lax.axis_size('blk'), axis=1))]
    split x0 -> x1, local copies, waits for them, and re-layouts: none -> 0.56 us  [body(): jnp.split(ordered, lax.axis_size('blk'), axis=1)]
  transfers between devices with their start and end apart: 1 -> 1, of which waited for: 1 -> 1; matrix products, arithmetic and copies ran while one was open for 6% -> 5% of each run, Pallas kernels for 0% -> 0%
where the time goes in v1:
time: 54.1 us; the launch traced here: 53.8 us
  other arithmetic  15.6 us (29%)
  local copies, waits for them, and re-layouts  13.2 us (24%)
  starting transfers between devices  8.34 us (15%)
  blocking collectives  6.97 us (13%)
  waiting for transfers between devices  6.68 us (12%)
  matrix products  2.15 us (4%)
  between operations  0.81 us (1%)
    unnamed x25, local copies, waits for them, and re-layouts  10.1 us
    all_to_all x1, starting transfers between devices, body(): lax.all_to_all(jnp.stack(jnp.split(ordered, lax.axis_size('blk'), axis=1)...  8.34 us
    all_to_all x1, waiting for transfers between devices, body(): lax.all_to_all(jnp.stack(jnp.split(ordered, lax.axis_size('blk'), axis=1)...  6.68 us
    another operation x3, other arithmetic, body(): factor = jnp.linalg.cholesky(gram_sum)  6.52 us
    another operation x2, other arithmetic, body(): new_basis = jax.scipy.linalg.solve_triangular(factor, image, lower=True)  6.16 us
    psum x1, blocking collectives, body(): gram_sum = lax.psum(gram_part, 'row')  3.57 us
    psum x1, blocking collectives, body(): projected = lax.psum(partial_proj, 'row')  3.41 us
    gather x1, local copies, waits for them, and re-layouts, body(): ordered = jnp.take(genotypes, assignment, axis=1)  1.31 us
  transfers between devices with their start and end apart: 1, of which 1 were waited for; matrix products, arithmetic and copies ran while one was open for 5% of the time, Pallas kernels for 0%

profile of v1, /device:TPU:0, one launch (start us, length us, event | category | flops | bytes accessed | tf_op | source)
XLA Modules:
  0.0 53.8 jit_solution(6985674774231968089)
XLA Ops:
  0.6 0.0 copy-start
  0.6 0.0 copy-start.3
  0.7 0.7 %compare_select_fusion = s32[16]{0:T(128)S(1)} fusion(s32[16]{0:T(128)} %param.5), kind=kLoop, calls=%fused_computation.49 | loop fusion | flops 48 | bytes 128 | tf_op jit(solution)/shard_map/jit(_take)/jit(_where)/select_n | solution.py:11
  1.4 0.0 copy-done.3
  1.4 0.2 copy-done
  1.6 1.3 %gather_fusion = bf16[16,8,1024]{2,0,1:T(8,128)(2,1)S(1)} fusion(bf16[8,16,1024]{2,1,0:T(8,128)(2,1)S(1)} %copy-done, s32[1024]{0:T(1024)S(1)} %pad_clamp_fusion), kind=kCustom, calls=%fused_computation | custom fusion | bytes 524352 | tf_op jit(solution)/shard_map/jit(_take)/gather | solution.py:11
  2.9 0.1 select_bitcast_fusion
  3.0 0.6 %fusion.21 = (bf16[8,1,1024]{2,1,0:T(2,128)(2,1)S(1)}, bf16[8,1,1024]{2,1,0:T(2,128)(2,1)S(1)}, bf16[8,1,1024]{2,1,0:T(2,128)(2,1)S(1)}, bf16[8,1,1024]{2,1,0:T(...) fusion(bf16[8,16,1024]{2,1,0:T(8,128)(2,1)S(1)} %select_bitcast, ...), kind=kLoop, calls=%fused_computation.57 | loop fusion | bytes 524288 | tf_op jit(solution)/shard_map/split | solution.py:13
  3.6 0.6 %constant_dynamic-update-slice_fusion.15 = bf16[16,8,1,1024]{3,1,2,0:T(8,128)(2,1)} fusion(bf16[8,1,1024]{2,1,0:T(2,128)(2,1)S(1)} %get-tuple-element.20), kind=kLoop, calls=%fused_computation.37 | loop fusion | bytes 32768
  4.2 0.6 %constant_dynamic-update-slice_fusion.14 = bf16[16,8,1,1024]{3,1,2,0:T(8,128)(2,1)} fusion(bf16[16,8,1,1024]{3,1,2,0:T(8,128)(2,1)} %constant_dynamic-update-slice_fusion.15, bf16[8,1,1024]{2,1,0:T(2,128)(2,1)S(1)} %get-tuple-element.19), kind=kLoop, calls=%fused_computation.36 | loop fusion | bytes 32768
  4.8 0.6 %constant_dynamic-update-slice_fusion.13 = bf16[16,8,1,1024]{3,1,2,0:T(8,128)(2,1)} fusion(bf16[16,8,1,1024]{3,1,2,0:T(8,128)(2,1)} %constant_dynamic-update-slice_fusion.14, bf16[8,1,1024]{2,1,0:T(2,128)(2,1)S(1)} %get-tuple-element.18), kind=kLoop, calls=%fused_computation.35 | loop fusion | bytes 32768
  5.4 0.6 %constant_dynamic-update-slice_fusion.12 = bf16[16,8,1,1024]{3,1,2,0:T(8,128)(2,1)} fusion(bf16[16,8,1,1024]{3,1,2,0:T(8,128)(2,1)} %constant_dynamic-update-slice_fusion.13, bf16[8,1,1024]{2,1,0:T(2,128)(2,1)S(1)} %get-tuple-element.17), kind=kLoop, calls=%fused_computation.34 | loop fusion | bytes 32768
  6.1 0.6 %constant_dynamic-update-slice_fusion.11 = bf16[16,8,1,1024]{3,1,2,0:T(8,128)(2,1)} fusion(bf16[16,8,1,1024]{3,1,2,0:T(8,128)(2,1)} %constant_dynamic-update-slice_fusion.12, bf16[8,1,1024]{2,1,0:T(2,128)(2,1)S(1)} %get-tuple-element.16), kind=kLoop, calls=%fused_computation.33 | loop fusion | bytes 32768
  6.7 0.6 %constant_dynamic-update-slice_fusion.10 = bf16[16,8,1,1024]{3,1,2,0:T(8,128)(2,1)} fusion(bf16[16,8,1,1024]{3,1,2,0:T(8,128)(2,1)} %constant_dynamic-update-slice_fusion.11, bf16[8,1,1024]{2,1,0:T(2,128)(2,1)S(1)} %get-tuple-element.15), kind=kLoop, calls=%fused_computation.32 | loop fusion | bytes 32768
  7.3 0.6 %constant_dynamic-update-slice_fusion.9 = bf16[16,8,1,1024]{3,1,2,0:T(8,128)(2,1)} fusion(bf16[16,8,1,1024]{3,1,2,0:T(8,128)(2,1)} %constant_dynamic-update-slice_fusion.10, bf16[8,1,1024]{2,1,0:T(2,128)(2,1)S(1)} %get-tuple-element.14), kind=kLoop, calls=%fused_computation.31 | loop fusion | bytes 32768
  7.9 0.6 %constant_dynamic-update-slice_fusion.8 = bf16[16,8,1,1024]{3,1,2,0:T(8,128)(2,1)} fusion(bf16[16,8,1,1024]{3,1,2,0:T(8,128)(2,1)} %constant_dynamic-update-slice_fusion.9, bf16[8,1,1024]{2,1,0:T(2,128)(2,1)S(1)} %get-tuple-element.13), kind=kLoop, calls=%fused_computation.30 | loop fusion | bytes 32768
  8.5 0.6 %constant_dynamic-update-slice_fusion.7 = bf16[16,8,1,1024]{3,1,2,0:T(8,128)(2,1)} fusion(bf16[16,8,1,1024]{3,1,2,0:T(8,128)(2,1)} %constant_dynamic-update-slice_fusion.8, bf16[8,1,1024]{2,1,0:T(2,128)(2,1)S(1)} %get-tuple-element.12), kind=kLoop, calls=%fused_computation.29 | loop fusion | bytes 32768
  9.1 0.6 %constant_dynamic-update-slice_fusion.6 = bf16[16,8,1,1024]{3,1,2,0:T(8,128)(2,1)} fusion(bf16[16,8,1,1024]{3,1,2,0:T(8,128)(2,1)} %constant_dynamic-update-slice_fusion.7, bf16[8,1,1024]{2,1,0:T(2,128)(2,1)S(1)} %get-tuple-element.11), kind=kLoop, calls=%fused_computation.28 | loop fusion | bytes 32768
  9.7 0.6 %constant_dynamic-update-slice_fusion.5 = bf16[16,8,1,1024]{3,1,2,0:T(8,128)(2,1)} fusion(bf16[16,8,1,1024]{3,1,2,0:T(8,128)(2,1)} %constant_dynamic-update-slice_fusion.6, bf16[8,1,1024]{2,1,0:T(2,128)(2,1)S(1)} %get-tuple-element.10), kind=kLoop, calls=%fused_computation.27 | loop fusion | bytes 32768
  10.3 0.6 %constant_dynamic-update-slice_fusion.4 = bf16[16,8,1,1024]{3,1,2,0:T(8,128)(2,1)} fusion(bf16[16,8,1,1024]{3,1,2,0:T(8,128)(2,1)} %constant_dynamic-update-slice_fusion.5, bf16[8,1,1024]{2,1,0:T(2,128)(2,1)S(1)} %get-tuple-element.9), kind=kLoop, calls=%fused_computation.26 | loop fusion | bytes 32768
  11.0 0.6 %constant_dynamic-update-slice_fusion.3 = bf16[16,8,1,1024]{3,1,2,0:T(8,128)(2,1)} fusion(bf16[16,8,1,1024]{3,1,2,0:T(8,128)(2,1)} %constant_dynamic-update-slice_fusion.4, bf16[8,1,1024]{2,1,0:T(2,128)(2,1)S(1)} %get-tuple-element.8), kind=kLoop, calls=%fused_computation.25 | loop fusion | bytes 32768
  11.6 0.6 %constant_dynamic-update-slice_fusion.2 = bf16[16,8,1,1024]{3,1,2,0:T(8,128)(2,1)} fusion(bf16[16,8,1,1024]{3,1,2,0:T(8,128)(2,1)} %constant_dynamic-update-slice_fusion.3, bf16[8,1,1024]{2,1,0:T(2,128)(2,1)S(1)} %get-tuple-element.7), kind=kLoop, calls=%fused_computation.24 | loop fusion | bytes 32768
  12.2 0.6 %constant_dynamic-update-slice_fusion.1 = bf16[16,8,1,1024]{3,1,2,0:T(8,128)(2,1)} fusion(bf16[16,8,1,1024]{3,1,2,0:T(8,128)(2,1)} %constant_dynamic-update-slice_fusion.2, bf16[8,1,1024]{2,1,0:T(2,128)(2,1)S(1)} %get-tuple-element.6), kind=kLoop, calls=%fused_computation.23 | loop fusion | bytes 32768
  12.8 0.6 %constant_dynamic-update-slice_fusion = bf16[16,8,1,1024]{3,1,2,0:T(8,128)(2,1)} fusion(bf16[16,8,1,1024]{3,1,2,0:T(8,128)(2,1)} %constant_dynamic-update-slice_fusion.1, bf16[8,1,1024]{2,1,0:T(2,128)(2,1)S(1)} %get-tuple-element.5), kind=kLoop, calls=%fused_computation.22 | loop fusion | bytes 32768 | tf_op jit(solution)/shard_map/stack | solution.py:13
  13.4 8.3 %all-to-all-start = ((bf16[16,8,1,1024]{3,1,2,0:T(8,128)(2,1)}), bf16[16,8,1,1024]{3,1,2,0:T(8,128)(2,1)S(1)}, u32[]{:S(2)}, u32[]{:S(2)}) async-start(bf16[16,8,1,1024]{3,1,2,0:T(8,128)(2,1)} %constant_dynamic-update-slice_fusion), calls=%async_computation | async-start | bytes 524288 | tf_op jit(solution)/shard_map/all_to_all | solution.py:13
  21.8 0.6 %dynamic_slice.3 = s32[1]{0:T(128)} dynamic-slice(s32[16]{0:T(128)S(1)} %copy-done.3, s32[]{:T(128)S(6)} %select_n.50), dynamic_slice_sizes={1} | dynamic-slice | bytes 12 | tf_op jit(solution)/shard_map/dynamic_slice | solution.py:19
  22.4 0.0 copy-start.4
  22.4 0.7 %copy-done.4 = s32[16]{0:T(128)S(1)} copy-done((s32[16]{0:T(128)S(1)}, s32[16]{0:T(128)}, u32[]{:S(2)}) %copy-start.4) | copy-done | bytes 88
  23.0 1.3 %fusion.18 = s32[]{:T(128)} fusion(s32[16]{0:T(128)S(1)} %copy-done.4, s32[]{:T(128)} %bitcast), kind=kLoop, calls=%fused_computation.54 | loop fusion | flops 47 | bytes 72 | tf_op jit(solution)/shard_map/reduce_sum | solution.py:21
  24.3 0.7 %add_compare_fusion = pred[1024]{0:T(1024)(128)(4,1)S(1)} fusion(s32[]{:T(128)} %fusion.18, s32[]{:T(128)S(6)} %mul.56), kind=kLoop, calls=%fused_computation.48 | loop fusion | flops 2048 | bytes 1032 | tf_op jit(solution)/shard_map/lt | solution.py:25
  24.9 0.0 copy-start.2
  25.0 6.7 %all-to-all-done = bf16[16,8,1,1024]{3,1,2,0:T(8,128)(2,1)S(1)} async-done(((bf16[16,8,1,1024]{3,1,2,0:T(8,128)(2,1)}), bf16[16,8,1,1024]{3,1,2,0:T(8,128)(2,1)S(1)}, u32[]{:S(2)}, u32[]{:S(2)}) %all-to-all-start) | async-done | bytes 262176 | tf_op jit(solution)/shard_map/all_to_all | solution.py:13
  31.6 0.1 convert_reduce_fusion
  31.7 0.1 fusion.8
  31.8 0.0 copy-done.2
  31.8 0.4 convolution_bitcast_fusion.2
  32.2 3.4 %psum.14 = f32[64,128]{1,0:T(8,128)S(1)} all-reduce(f32[64,128]{1,0:T(8,128)S(1)} %convolution_bitcast_fusion.2), channel_id=1, replica_groups=mesh['blk'=16,'row'=2] {'row'}, use_global_device_ids=true, to_apply=%region_3.4 | all-reduce | flops 8192 | bytes 65536 | tf_op jit(solution)/shard_map/psum | solution.py:41
  35.6 0.3 fusion.1
  35.9 0.0 copy-start.1
  35.9 0.4 convolution_bitcast_fusion.1
  36.3 3.6 %psum.15 = f32[1,64,64]{1,2,0:T(8,128)S(1)} all-reduce(f32[1,64,64]{1,2,0:T(8,128)S(1)} %convolution_bitcast_fusion.1), channel_id=1, replica_groups=mesh['blk'=16,'row'=2] {'row'}, use_global_device_ids=true, to_apply=%region_4.5 | all-reduce | flops 4096 | bytes 32768 | tf_op jit(solution)/shard_map/psum | solution.py:56
  39.9 0.1 copy.160
  40.0 5.8 %custom-call.8 = f32[1,64,64]{2,1,0:T(8,128)S(1)} custom-call(f32[1,64,64]{2,1,0:T(8,128)S(1)} %fusion.16), custom_call_target="Cholesky" | custom-call | tf_op jit(solution)/shard_map/jit(cholesky)/cholesky | solution.py:57
  45.8 0.6 %compare_reduce_fusion = pred[]{:T(512)} fusion(f32[64]{0:T(128)S(1)} %select_reduce_fusion), kind=kLoop, calls=%fused_computation.51 | loop fusion | flops 127 | bytes 257 | tf_op jit(solution)/shard_map/jit(cholesky)/cholesky | solution.py:57
  46.5 1.3 %fusion.17 = (f32[1,64,64]{2,1,0:T(8,128)S(1)}, f32[1,64,64]{2,1,0:T(8,128)}) fusion(f32[1,64,64]{2,1,0:T(8,128)S(1)} %custom-call.8, pred[]{:T(512)} %compare_reduce_fusion), kind=kLoop, calls=%fused_computation.45 | loop fusion | flops 16384 | bytes 49153 | tf_op jit(solution)/shard_map/jit(_solve_triangular)/triangular_solve | solution.py:58
  47.7 4.9 %custom-call.9 = f32[1,64,64]{1,2,0:T(8,128)S(1)} custom-call(f32[1,64,64]{2,1,0:T(8,128)S(1)} %get-tuple-element.3), custom_call_target="InvertDiagBlocksLowerTriangular" | custom-call | tf_op jit(solution)/shard_map/jit(_solve_triangular)/triangular_solve | solution.py:58
  52.6 0.0 copy-done.1
  52.7 1.1 %convolution_bitcast_fusion = f32[1,64,1024]{2,1,0:T(8,128)} fusion(f32[1,64,1024]{2,1,0:T(8,128)S(1)} %fusion.1, f32[1,64,64]{1,2,0:T(8,128)S(1)} %custom-call.9), kind=kOutput, calls=%fused_computation.3 | convolution fusion | flops 50331648 | bytes 540672 | tf_op jit(solution)/shard_map/jit(_solve_triangular)/triangular_solve | solution.py:58
  (6 shorter events, 0.1 us)
Async XLA Ops:
  0.6 1.0 %copy-start = (bf16[8,16,1024]{2,1,0:T(8,128)(2,1)S(1)}, bf16[8,16,1024]{2,1,0:T(8,128)(2,1)}, u32[]{:S(2)}) copy-start(bf16[8,16,1024]{2,1,0:T(8,128)(2,1)} %param.4) | copy-start | bytes 786436
  0.6 0.7 %copy-start.3 = (s32[16]{0:T(128)S(1)}, s32[16]{0:T(128)}, u32[]{:S(2)}) copy-start(s32[16]{0:T(128)} %param.5) | copy-start | bytes 196
  13.4 18.2 %all-to-all-start = ((bf16[16,8,1,1024]{3,1,2,0:T(8,128)(2,1)}), bf16[16,8,1,1024]{3,1,2,0:T(8,128)(2,1)S(1)}, u32[]{:S(2)}, u32[]{:S(2)}) async-start(bf16[16,8,1,1024]{3,1,2,0:T(8,128)(2,1)} %constant_dynamic-update-slice_fusion), calls=%async_computation | async-start | bytes 524288 | tf_op jit(solution)/shard_map/all_to_all | solution.py:13
  22.4 0.7 %copy-start.4 = (s32[16]{0:T(128)S(1)}, s32[16]{0:T(128)}, u32[]{:S(2)}) copy-start(s32[16]{0:T(128)} %param.6) | copy-start | bytes 196
  24.9 6.9 %copy-start.2 = (f32[1,64,1024]{2,1,0:T(8,128)S(1)}, f32[1,64,1024]{2,1,0:T(8,128)}, u32[]{:S(2)}) copy-start(f32[1,64,1024]{2,1,0:T(8,128)} %param.7) | copy-start | bytes 786436
  35.9 16.8 %copy-start.1 = (f32[1,64,1024]{2,1,0:T(8,128)}, f32[1,64,1024]{2,1,0:T(8,128)S(1)}, u32[]{:S(2)}) copy-start(f32[1,64,1024]{2,1,0:T(8,128)S(1)} %fusion.1) | copy-start | bytes 786436
